TPU v7x, 32 devices: a whole 2x2x4 slice. The times are simulated.
32 devices in a mesh: rows: 4 (over z), cols: 4 (over y, x), space: 2 (over core).
Axes of the slice: x: 2, y: 2, z: 4, core: 2. Of those that a mesh axis runs over, the one named last changes fastest.
Arguments:
- hamiltonian: float32 [2048, 1536], P(('rows', 'cols', 'space')), may hold values from -1 to 1
- correlation_root: float32 [2048, 1536], P('rows'), may hold values from -1 to 2
- pattern: int32 [64, 48], replicated, may hold values from 0 to 1
- sub_blocks: int32 [64, 16], P(('rows', 'cols', 'space')), may hold values from 0 to 47, as said below
- sub_count: int32 [64], P(('rows', 'cols', 'space')), may hold values from 8 to 16, as said below
Outputs:
- density: float32 [2048, 1536], P(('rows', 'cols', 'space'))
- charges: float32 [2048], P(('rows', 'cols', 'space'))
Inputs may be any that keep to these rules, and one draw needn't show every extreme that they name: `sub_blocks`: row g lists distinct positions; its first entry is 16 + g mod 16, the position of block g itself. `sub_count`: some submatrix has exactly 16 live blocks.
All inputs are finite; a program needn't handle non-finite values.
Results may differ from a plain program's by a relative error of at most 0.0003.
Values sent between devices are 32-bit elements; how exact they have to be, the bound alone decides.
A program may use at most 128 MiB of HBM per device.

v0:
```python
import functools

import jax
import jax.numpy as jnp
from jax import lax
from jax.experimental import pallas as pl
from jax.experimental.pallas import tpu as pltpu
from jax.sharding import PartitionSpec as P

BLK = 32
GROUP = ("cols", "space")


def multiply_nt(leftside, rightside):
    return lax.dot_general(
        leftside,
        rightside,
        (((1,), (1,)), ((), ())),
        precision=lax.Precision.HIGH,
        preferred_element_type=jnp.float32,
    )


class Sender:
    def __init__(self, send_sems, recv_sems):
        self.sems = (send_sems, recv_sems)
        self.copies = []

    def start(self, source, target, device):
        slot = len(self.copies)
        copy = pltpu.make_async_remote_copy(
            src_ref=source,
            dst_ref=target,
            send_sem=self.sems[0].at[slot],
            recv_sem=self.sems[1].at[slot],
            device_id=device,
            device_id_type=pl.DeviceIdType.MESH,
        )
        copy.start()
        self.copies.append(copy)
        return copy

    def finish(self):
        for copy in self.copies:
            copy.wait_send()


class Gather:
    def __init__(self, sender, source, out_ref, rows, lanes):
        self.sender, self.out_ref, self.rows, self.lanes = sender, out_ref, rows, lanes
        col = lax.axis_index("cols")
        space = lax.axis_index("space")
        self.first = col + 1 - 2 * lax.rem(col, 2)
        self.second = lax.rem(col + 2, 4)
        self.third = lax.rem(self.first + 2, 4)
        self.space = space
        own = self.region(col)
        self.from_first = sender.start(source, own, {"cols": self.first})
        self.from_second = sender.start(source, own, {"cols": self.second})
        self.pending = [sender.start(source, own, {"space": 1 - space})]

    def region(self, col, half=None):
        start, size = self.rows
        if half is not None:
            size = size // 2
            start = start + half * size
        owner = col * 2 + self.space
        return self.out_ref.at[owner, pl.ds(start, size), pl.ds(*self.lanes)]

    def partner(self, region):
        self.pending.append(self.sender.start(region, region, {"space": 1 - self.space}))

    def relay(self):
        self.from_first.wait_recv()
        passed = self.region(self.first, 1)
        self.half_second = self.sender.start(passed, passed, {"cols": self.second})
        self.partner(self.region(self.first))
        self.from_second.wait_recv()
        passed = self.region(self.second, 0)
        self.half_first = self.sender.start(passed, passed, {"cols": self.first})
        self.partner(self.region(self.second))

    def last_hop(self):
        self.half_second.wait_recv()
        self.partner(self.region(self.third, 1))
        self.half_first.wait_recv()
        self.partner(self.region(self.third, 0))

    def finish(self):
        for copy in self.pending:
            copy.wait_recv()


def meet(along_rows, in_slab):
    barrier = pltpu.get_barrier_semaphore()
    devices = []
    if along_rows:
        row = lax.axis_index("rows")
        count = lax.axis_size("rows")
        devices += [{"rows": lax.rem(row + 1, count)}, {"rows": lax.rem(row + count - 1, count)}]
    if in_slab:
        col = lax.axis_index("cols")
        devices += [{"cols": col + 1 - 2 * lax.rem(col, 2)}, {"cols": lax.rem(col + 2, 4)}]
        devices += [{"space": 1 - lax.axis_index("space")}]
    for device in devices:
        pl.semaphore_signal(barrier, inc=1, device_id=device, device_id_type=pl.DeviceIdType.MESH)
    pl.semaphore_wait(barrier, len(devices))


def send_panels(sender, piece_ref, window_ref):
    row = lax.axis_index("rows")
    count = lax.axis_size("rows")
    height, slab = piece_ref.shape
    own = height // 3
    above = sender.start(
        piece_ref.at[pl.ds(own, 2 * own), :],
        window_ref.at[pl.ds(0, 2 * own), pl.ds(0, slab)],
        {"rows": lax.rem(row + 1, count)},
    )
    below = sender.start(
        piece_ref.at[pl.ds(0, 2 * own), :],
        window_ref.at[pl.ds(own, 2 * own), pl.ds(2 * slab, slab)],
        {"rows": lax.rem(row + count - 1, count)},
    )
    return above, below


def fill_rest(piece_ref, window_ref, slab, own):
    zero = jnp.zeros((own, slab), jnp.float32)
    window_ref[2 * own :, :slab] = zero
    window_ref[:own, 2 * slab :] = zero


def exchange_kernel(piece_ref, window_ref, send_sems, recv_sems):
    meet(True, False)
    sender = Sender(send_sems, recv_sems)
    copies = send_panels(sender, piece_ref, window_ref)
    height, slab = piece_ref.shape
    window_ref[:, slab : 2 * slab] = piece_ref[...]
    fill_rest(piece_ref, window_ref, slab, height // 3)
    for copy in copies:
        copy.wait_recv()
    sender.finish()


def gather_kernel(block_ref, out_ref, send_sems, recv_sems):
    meet(False, True)
    sender = Sender(send_sems, recv_sems)
    height, width = block_ref.shape
    gather = Gather(sender, block_ref, out_ref, (0, height), (0, width))
    out_ref[lax.axis_index(GROUP)] = block_ref[...]
    gather.relay()
    gather.last_hop()
    gather.finish()
    sender.finish()


def both_kernel(piece_ref, block_ref, window_ref, out_ref, send_sems, recv_sems):
    meet(True, True)
    sender = Sender(send_sems, recv_sems)
    copies = send_panels(sender, piece_ref, window_ref)
    height, width = block_ref.shape
    gather = Gather(sender, block_ref, out_ref, (0, height), (0, width))
    out_ref[lax.axis_index(GROUP)] = block_ref[...]
    height, slab = piece_ref.shape
    window_ref[:, slab : 2 * slab] = piece_ref[...]
    fill_rest(piece_ref, window_ref, slab, height // 3)
    gather.relay()
    gather.last_hop()
    gather.finish()
    for copy in copies:
        copy.wait_recv()
    sender.finish()


def window_kernel(piece_ref, out_ref, send_sems, recv_sems):
    meet(True, True)
    sender = Sender(send_sems, recv_sems)
    height, slab = piece_ref.shape
    own = height // 3
    home = lax.axis_index(GROUP)
    above, below = send_panels(sender, piece_ref, out_ref.at[home])
    gathers = [Gather(sender, piece_ref, out_ref, (0, height), (slab, slab))]
    out_ref[home, :, slab : 2 * slab] = piece_ref[...]
    zero = jnp.zeros((own, slab), jnp.float32)
    for owner in range(out_ref.shape[0]):
        out_ref[owner, 2 * own :, :slab] = zero
        out_ref[owner, :own, 2 * slab :] = zero
    for copy, start, lane in ((above, 0, 0), (below, own, 2 * slab)):
        copy.wait_recv()
        source = out_ref.at[home, pl.ds(start, 2 * own), pl.ds(lane, slab)]
        gathers.append(Gather(sender, source, out_ref, (start, 2 * own), (lane, slab)))
    for gather in gathers:
        gather.relay()
    for gather in gathers:
        gather.last_hop()
    for gather in gathers:
        gather.finish()
    sender.finish()


def exchange_call(kernel, copies, collective, shapes, *operands):
    space = pl.BlockSpec(memory_space=pltpu.VMEM)
    return pl.pallas_call(
        kernel,
        out_shape=[jax.ShapeDtypeStruct(shape, jnp.float32) for shape in shapes],
        in_specs=[space] * len(operands),
        out_specs=[space] * len(shapes),
        scratch_shapes=[pltpu.SemaphoreType.DMA((copies,)), pltpu.SemaphoreType.DMA((copies,))],
        compiler_params=pltpu.CompilerParams(
            collective_id=collective, has_side_effects=True, vmem_limit_bytes=40 * 2**20
        ),
    )(*operands)


def split(value):
    upper = value.astype(jnp.bfloat16)
    return upper, (value - upper.astype(jnp.float32)).astype(jnp.bfloat16)


def dot_f32(leftside, rightside):
    return jnp.dot(leftside, rightside, preferred_element_type=jnp.float32)


def dot_split(leftside, rightside):
    left_hi, left_lo = leftside
    right_hi, right_lo = rightside
    return (
        dot_f32(left_hi, right_hi)
        + dot_f32(left_hi, right_lo)
        + dot_f32(left_lo, right_hi)
    )


def submatrix_kernel(maxb, slab_blocks, pos_ref, count_ref, offs_ref, gathered_ref, out_ref, rows_ref):
    width = gathered_ref.shape[1] // 3
    slab = gathered_ref.shape[2] // 3
    per_piece = width // BLK
    index = pl.program_id(0)
    live = count_ref[index]

    def place(p, carry):
        block = pos_ref[index, p]
        panel = block // slab_blocks
        within = lax.rem(block, slab_blocks)
        owner = within // per_piece
        start = pl.multiple_of(panel * width + lax.rem(within, per_piece) * BLK, BLK)
        target = pl.multiple_of(p * BLK, BLK)
        values = gathered_ref[owner, pl.ds(start, BLK), :]
        rows_ref[pl.ds(target, BLK), :] = jnp.where(p < live, values, 0.0)
        return carry

    lax.fori_loop(0, maxb, place, 0)
    offsets = offs_ref[0]
    order = maxb * BLK
    select = lax.broadcasted_iota(jnp.int32, (3 * slab, order), 0) == offsets
    select = jnp.where(select, 1.0, 0.0).astype(jnp.bfloat16)
    rows_hi, rows_lo = split(rows_ref[...])
    assembled = dot_f32(rows_hi, select) + dot_f32(rows_lo, select)
    columns = lax.broadcasted_iota(jnp.int32, (order, order), 1)
    assembled = jnp.where(columns < live * BLK, assembled, 0.0)
    symmetric = 0.5 * (assembled + assembled.T)
    total = jnp.sum(jnp.sum(symmetric * symmetric, axis=1, keepdims=True), axis=0, keepdims=True)
    live_order = jnp.full((1, 1), live * BLK, jnp.int32).astype(jnp.float32)
    iterate = symmetric * (jnp.sqrt(live_order) / (2.0 * jnp.sqrt(total + 1e-06)))
    parts = split(iterate)
    square = split(dot_split(parts, parts))
    iterate = 1.5 * iterate - 0.5 * dot_split(parts, square)
    home = iterate[:BLK]
    parts = split(iterate)
    once = dot_split((parts[0][:BLK], parts[1][:BLK]), parts)
    home = 1.5 * home - 0.5 * dot_split(split(once), parts)
    row = lax.broadcasted_iota(jnp.int32, (BLK, order), 0)
    column = lax.broadcasted_iota(jnp.int32, (BLK, order), 1)
    density = 0.5 * (jnp.where(row == column, 1.0, 0.0) - home)
    density_hi, density_lo = split(density)
    spread = functools.partial(
        lax.dot_general,
        dimension_numbers=(((1,), (1,)), ((), ())),
        preferred_element_type=jnp.float32,
    )
    out_ref[...] = spread(density_hi, select) + spread(density_lo, select)


def submatrices(gathered, sub_blocks, sub_count):
    own_blocks, maxb = sub_blocks.shape
    slab = gathered.shape[2] // 3
    order = maxb * BLK
    offsets = sub_blocks[:, :, None] * BLK + jnp.arange(BLK, dtype=jnp.int32)
    offsets = offsets.reshape(own_blocks, 1, order)
    return pl.pallas_call(
        functools.partial(submatrix_kernel, maxb, slab // BLK),
        out_shape=jax.ShapeDtypeStruct((own_blocks * BLK, 3 * slab), jnp.float32),
        grid_spec=pltpu.PrefetchScalarGridSpec(
            num_scalar_prefetch=2,
            grid=(own_blocks,),
            in_specs=[
                pl.BlockSpec((1, 1, order), lambda i, *_: (i, 0, 0)),
                pl.BlockSpec(memory_space=pltpu.VMEM),
            ],
            out_specs=pl.BlockSpec((BLK, 3 * slab), lambda i, *_: (i, 0)),
            scratch_shapes=[pltpu.VMEM((order, 3 * slab), jnp.float32)],
        ),
    )(sub_blocks, sub_count, offsets, gathered)


def shards(hamiltonian, correlation_root, pattern, sub_blocks, sub_count):
    slab = correlation_root.shape[0]
    slab_blocks = slab // BLK
    own = hamiltonian.shape[0]
    parts = slab // own
    slab_index = lax.axis_index("rows")
    home = lax.axis_index(GROUP)
    slab_pattern = lax.dynamic_slice_in_dim(pattern, slab_index * slab_blocks, slab_blocks, 0)
    weights = slab_pattern.astype(jnp.float32)
    own_pattern = lax.dynamic_slice_in_dim(weights, home * (own // BLK), own // BLK, 0)
    own_mask = jnp.repeat(jnp.repeat(own_pattern, BLK, axis=0), BLK, axis=1)
    piece_pattern = lax.dynamic_index_in_dim(
        weights.reshape(slab_blocks, 3, parts, own // BLK), home, 2, keepdims=False
    )
    piece_mask = jnp.repeat(jnp.repeat(piece_pattern.transpose(1, 2, 0), BLK, axis=1), BLK, axis=2)
    piece_mask = piece_mask.reshape(3 * own, slab)

    root_piece = lax.dynamic_index_in_dim(
        correlation_root.reshape(slab, 3, parts, own), home, 2, keepdims=False
    ).transpose(1, 2, 0).reshape(3 * own, slab)
    window_shape = (3 * own, 3 * slab)
    block_shape = (parts, own, 3 * slab)
    root_window, whole_hamiltonian = exchange_call(
        both_kernel, 11, 1, [window_shape, block_shape], root_piece, hamiltonian
    )

    def step(left, window):
        return piece_mask * multiply_nt(window, left.reshape(slab, 3 * slab))

    half_done = step(whole_hamiltonian, root_window)
    (done_window,) = exchange_call(exchange_kernel, 2, 2, [window_shape], half_done)
    ortho = step(correlation_root, done_window)
    (gathered,) = exchange_call(window_kernel, 29, 3, [(parts, *window_shape)], ortho)
    home_density = submatrices(gathered, sub_blocks, sub_count)
    (whole_density,) = exchange_call(gather_kernel, 9, 4, [block_shape], home_density)
    half_back = step(whole_density, root_window)
    (back_window,) = exchange_call(exchange_kernel, 2, 5, [window_shape], half_back)
    density = multiply_nt(back_window, correlation_root).reshape(3, own, parts, own)
    density = lax.all_to_all(density.transpose(2, 3, 0, 1), GROUP, 0, 0, tiled=False)
    density = own_mask * density.transpose(1, 2, 0, 3).reshape(own, 3 * slab)
    return density, jnp.sum(density, axis=1)


def solution(mesh):
    return jax.shard_map(
        shards,
        mesh=mesh,
        in_specs=(
            P(("rows", "cols", "space"), None),
            P("rows", None),
            P(),
            P(("rows", "cols", "space"), None),
            P(("rows", "cols", "space")),
        ),
        out_specs=(P(("rows", "cols", "space"), None), P(("rows", "cols", "space"))),
        check_vma=False,
    )
```

profile of v0, /device:TPU:0, one launch (start us, length us, event | category | flops | bytes accessed | tf_op | source)
XLA Modules:
  0.0 160.8 jit_solution(14152988122888022578)
XLA Ops:
  0.6 0.8 dynamic-slice_convert_fusion
  1.5 0.1 copy.33
  1.6 0.1 broadcast_in_dim.18
  1.7 0.1 reshape.76
  1.8 0.1 broadcast_in_dim.19
  1.9 0.6 reshape_reshape.3
  2.5 0.2 copy.38
  2.7 0.0 copy-start.2
  2.7 3.6 %copy.35 = f32[512,1536]{0,1:T(8,128)} copy(f32[512,1536]{1,0:T(8,128)} %param.6) | data formatting | bytes 6291456 | tf_op args[1]
  6.3 1.0 constant_dynamic-slice_fusion
  7.3 0.0 copy-done.2
  7.3 22.5 %shard_map.68 = (f32[192,1536]{1,0:T(8,128)S(1)}, f32[8,64,1536]{2,1,0:T(8,128)S(1)}) custom-call(f32[192,512]{1,0:T(8,128)S(1)} %bitcast.51, f32[64,1536]{1,0:T(8,128)S(1)} %copy-done.2), custom_call_target="tpu_custom_call" | custom-call | tf_op jit(solution)/shard_map/pallas_call | solution.py:204
  29.9 0.0 copy-start.3
  29.9 1.7 %convolution_multiply_fusion.2.piece_ref = f32[192,512]{1,0:T(8,128)S(1)} fusion(f32[192,512]{1,0:T(8,128)S(1)} %copy.38, f32[192,1536]{1,0:T(8,128)S(1)} %get-tuple-element.4, f32[512,1536]{1,0:T(8,128)S(1)} %bitcast.50), kind=kOutput, calls=%fused_computation.2 | convolution fusion | flops 906067968 | bytes 5111808 | tf_op jit(solution)/shard_map/dot_general | solution.py:15
  31.6 14.3 %shard_map.69 = f32[192,1536]{1,0:T(8,128)S(1)} custom-call(f32[192,512]{1,0:T(8,128)S(1)} %convolution_multiply_fusion.2.piece_ref), custom_call_target="tpu_custom_call" | custom-call | tf_op jit(solution)/shard_map/pallas_call | solution.py:204
  45.9 0.0 copy-done.3
  45.9 1.7 %convolution_multiply_fusion.1.piece_ref = f32[192,512]{1,0:T(8,128)S(1)} fusion(f32[192,512]{1,0:T(8,128)S(1)} %copy.38, f32[192,1536]{1,0:T(8,128)S(1)} %shard_map.69, f32[512,1536]{1,0:T(8,128)S(1)} %copy-done.3), kind=kOutput, calls=%fused_computation.1 | convolution fusion | flops 906067968 | bytes 5111808 | tf_op jit(solution)/shard_map/dot_general | solution.py:15
  47.6 0.0 copy-start.5
  47.6 35.1 %shard_map.70.gathered_ref = f32[8,192,1536]{2,1,0:T(8,128)S(1)} custom-call(f32[192,512]{1,0:T(8,128)S(1)} %convolution_multiply_fusion.1.piece_ref), custom_call_target="tpu_custom_call" | custom-call | tf_op jit(solution)/shard_map/pallas_call | solution.py:204
  82.7 3.6 %copy-done = f32[8,192,1536]{2,1,0:T(8,128)} copy-done((f32[8,192,1536]{2,1,0:T(8,128)}, f32[8,192,1536]{2,1,0:T(8,128)S(1)}, u32[]{:S(2)}) %copy-start) | copy-done | bytes 9437208
  86.4 0.1 add.45
  86.4 0.1 add.46
  86.5 0.1 add.48
  86.6 0.6 broadcast_add_fusion.offs_ref
  87.2 18.4 %shard_map.71.block_ref = f32[64,1536]{1,0:T(8,128)} custom-call(s32[2,16]{1,0:T(2,128)} %pos_ref.1, s32[2]{0:T(128)} %count_ref.1, s32[2,1,512]{2,1,0:T(1,128)} %broadcast_add_fusion.offs_ref, f32[8,192,1536]{2,1,0:T(8,128)} %copy-done), custom_call_target="tpu_custom_call" | custom-call | tf_op jit(solution)/shard_map/pallas_call | solution.py:291
  105.6 1.0 copy-done.1
  106.6 19.0 %shard_map.72 = f32[8,64,1536]{2,1,0:T(8,128)S(1)} custom-call(f32[64,1536]{1,0:T(8,128)S(1)} %copy-done.1), custom_call_target="tpu_custom_call" | custom-call | tf_op jit(solution)/shard_map/pallas_call | solution.py:204
  125.5 0.0 copy-start.4
  125.5 1.7 %convolution_multiply_fusion.piece_ref = f32[192,512]{1,0:T(8,128)S(1)} fusion(f32[192,512]{1,0:T(8,128)S(1)} %copy.38, f32[192,1536]{1,0:T(8,128)S(1)} %get-tuple-element.4, f32[512,1536]{1,0:T(8,128)S(1)} %bitcast.49), kind=kOutput, calls=%fused_computation | convolution fusion | flops 906067968 | bytes 5111808 | tf_op jit(solution)/shard_map/dot_general | solution.py:15
  127.2 14.3 %shard_map.73 = f32[192,1536]{1,0:T(8,128)S(1)} custom-call(f32[192,512]{1,0:T(8,128)S(1)} %convolution_multiply_fusion.piece_ref), custom_call_target="tpu_custom_call" | custom-call | tf_op jit(solution)/shard_map/pallas_call | solution.py:204
  141.5 0.0 copy-done.4
  141.5 1.7 %fusion.2 = f32[192,512]{1,0:T(8,128)S(1)} fusion(f32[192,1536]{1,0:T(8,128)S(1)} %shard_map.73, f32[512,1536]{1,0:T(8,128)S(1)} %copy-done.4), kind=kOutput, calls=%fused_computation.14 | convolution fusion | flops 905969664 | bytes 4718592 | tf_op jit(solution)/shard_map/dot_general | solution.py:15
  143.2 0.2 reshape.81
  143.4 0.2 copy.47
  143.6 1.2 reshape.83
  144.8 3.5 %all-to-all-start = ((f32[8,1,12288]{2,1,0:T(1,128)}), f32[8,1,12288]{2,1,0:T(1,128)S(1)}, u32[]{:S(2)}, u32[]{:S(2)}) async-start(f32[8,1,12288]{2,1,0:T(1,128)} %reshape.83), calls=%async_computation | async-start | bytes 786432 | tf_op jit(solution)/shard_map/all_to_all | solution.py:345
  148.3 0.1 constant_dynamic-slice_fusion.1
  148.3 0.1 copy.30
  148.4 0.1 copy.31
  148.5 8.0 %all-to-all-done = f32[8,1,12288]{2,1,0:T(1,128)S(1)} async-done(((f32[8,1,12288]{2,1,0:T(1,128)}), f32[8,1,12288]{2,1,0:T(1,128)S(1)}, u32[]{:S(2)}, u32[]{:S(2)}) %all-to-all-start) | async-done | bytes 393248 | tf_op jit(solution)/shard_map/all_to_all | solution.py:345
  156.5 0.5 broadcast.19
  157.0 1.6 reduce.2
  158.6 0.3 reshape.84
  158.9 0.1 copy.40
  159.0 0.1 bitcast_multiply_fusion
  159.0 1.0 copy.41
  160.0 0.1 broadcast_in_dim.17
  160.1 0.8 fusion
  (8 shorter events, 0.0 us)
Async XLA Ops:
  2.7 4.6 %copy-start.2 = (f32[64,1536]{1,0:T(8,128)S(1)}, f32[64,1536]{1,0:T(8,128)}, u32[]{:S(2)}) copy-start(f32[64,1536]{1,0:T(8,128)} %block_ref.1) | copy-start | bytes 1179652
  29.9 16.0 %copy-start.3 = (f32[512,1536]{1,0:T(8,128)S(1)}, f32[512,1536]{1,0:T(8,128)}, u32[]{:S(2)}) copy-start(f32[512,1536]{1,0:T(8,128)} %param.6) | copy-start | bytes 9437188
  47.6 38.8 %copy-start.5 = (s32[2,16]{1,0:T(2,128)S(1)}, s32[2,16]{1,0:T(2,128)}, u32[]{:S(2)}) copy-start(s32[2,16]{1,0:T(2,128)} %pos_ref.1) | copy-start | bytes 388
  82.7 3.6 %copy-start = (f32[8,192,1536]{2,1,0:T(8,128)}, f32[8,192,1536]{2,1,0:T(8,128)S(1)}, u32[]{:S(2)}) copy-start(f32[8,192,1536]{2,1,0:T(8,128)S(1)} %shard_map.70.gathered_ref) | copy-start | bytes 28311556
  105.6 1.0 copy-start.1
  125.5 16.0 %copy-start.4 = (f32[512,1536]{1,0:T(8,128)S(1)}, f32[512,1536]{1,0:T(8,128)}, u32[]{:S(2)}) copy-start(f32[512,1536]{1,0:T(8,128)} %param.6) | copy-start | bytes 9437188
  144.8 11.7 %all-to-all-start = ((f32[8,1,12288]{2,1,0:T(1,128)}), f32[8,1,12288]{2,1,0:T(1,128)S(1)}, u32[]{:S(2)}, u32[]{:S(2)}) async-start(f32[8,1,12288]{2,1,0:T(1,128)} %reshape.83), calls=%async_computation | async-start | bytes 786432 | tf_op jit(solution)/shard_map/all_to_all | solution.py:345
where the time goes:
time: 161 us
  Pallas kernels  124 us (77%)
  local copies, waits for them, and re-layouts  14.4 us (9%)
  waiting for transfers between devices  8.01 us (5%)
  matrix products  6.8 us (4%)
  other arithmetic  3.81 us (2%)
  starting transfers between devices  3.45 us (2%)
    pallas_call x5, Pallas kernels, exchange_call(): pl.pallas_call(kernel, out_shape=[jax.ShapeDtypeStruct(shape, jnp.float32...  105 us
    pallas_call x1, Pallas kernels, submatrices(): pl.pallas_call(functools.partial(submatrix_kernel, maxb, slab // BLK), ou...  18.4 us
    unnamed x16, local copies, waits for them, and re-layouts  10.8 us
    all_to_all x1, waiting for transfers between devices, shards(): lax.all_to_all(density.transpose(2, 3, 0, 1), GROUP, 0, 0, tiled=False)  8.01 us
    dot_general x4, matrix products, multiply_nt(): lax.dot_general(leftside, rightside, (((1,), (1,)), ((), ())), precision=...  6.8 us
    all_to_all x1, starting transfers between devices, shards(): lax.all_to_all(density.transpose(2, 3, 0, 1), GROUP, 0, 0, tiled=False)  3.45 us
  transfers between devices with their start and end apart: 1, of which 1 were waited for; matrix products, arithmetic and copies ran while one was open for 0% of the time, Pallas kernels for 0%

commit v1 on v0

v1 whole, which is shorter than its diff:
```python
import functools

import jax
import jax.numpy as jnp
from jax import lax
from jax.experimental import pallas as pl
from jax.experimental.pallas import tpu as pltpu
from jax.sharding import PartitionSpec as P

BLK = 32
F32 = jnp.float32
BF16 = jnp.bfloat16


def split(value):
    upper = value.astype(BF16)
    return upper, (value - upper.astype(F32)).astype(BF16)


def dot(leftside, rightside):
    return jnp.dot(leftside, rightside, preferred_element_type=F32)


def product(stacked, right):
    high, low = right
    half = stacked.shape[0] // 2
    both = dot(stacked, high)
    return both[:half] + both[half:] + dot(stacked[:half], low)


def stack(value):
    return jnp.concatenate(split(value), axis=0)


def combine(above, own, below, width):
    return jnp.concatenate(
        [
            above[:, :width] + own[:, :width],
            above[:, width:] + own[:, width : 2 * width] + below[:, :width],
            own[:, 2 * width :] + below[:, width:],
        ],
        axis=1,
    )


class Sender:
    def __init__(self, send_sems, recv_sems):
        self.sems = (send_sems, recv_sems)
        self.copies = []

    def __call__(self, source, target, device):
        slot = len(self.copies)
        copy = pltpu.make_async_remote_copy(
            src_ref=source,
            dst_ref=target,
            send_sem=self.sems[0].at[slot],
            recv_sem=self.sems[1].at[slot],
            device_id=device,
            device_id_type=pl.DeviceIdType.MESH,
        )
        copy.start()
        self.copies.append(copy)
        return copy

    def finish(self):
        for copy in self.copies:
            copy.wait_send()


def kernel(
    pos_ref,
    count_ref,
    ham_ref,
    root_ref,
    pattern_ref,
    density_ref,
    charges_ref,
    root_v,
    left_s,
    ham_v,
    land_v,
    wide_hi,
    wide_lo,
    near_hi,
    near_lo,
    mask_a,
    mask_b,
    half_v,
    back_v,
    ortho_v,
    acc_v,
    sub_v,
    band_v,
    rows_v,
    strip_v,
    final_v,
    local_sems,
    send_sems,
    recv_sems,
):
    row = lax.axis_index("rows")
    count = lax.axis_size("rows")
    col = lax.axis_index("cols")
    space = lax.axis_index("space")
    cols = lax.axis_size("cols")
    slab, window = root_v.shape
    own = ham_ref.shape[0]
    chunk = slab // cols
    half = slab // 2
    maxb = pos_ref.shape[1]
    slab_blocks = slab // BLK
    own_blocks = own // BLK
    order = maxb * BLK
    groups = chunk // BLK

    first = col + 1 - 2 * lax.rem(col, 2)
    second = lax.rem(col + 2, 4)
    third = lax.rem(first + 2, 4)
    above = lax.rem(row + 1, count)
    below = lax.rem(row + count - 1, count)
    up, down = {"rows": above}, {"rows": below}
    side, cross, mate = {"cols": first}, {"cols": second}, {"space": 1 - space}
    lanes = pl.ds(pl.multiple_of(chunk * col, chunk), chunk)

    load_root = pltpu.make_async_copy(root_ref, root_v, local_sems.at[0])
    load_ham = pltpu.make_async_copy(ham_ref, ham_v.at[col], local_sems.at[1])
    load_root.start()
    load_ham.start()

    barrier = pltpu.get_barrier_semaphore()
    peers = [mate]
    for offset in range(cols):
        other = lax.rem(col + offset, cols)
        peers += [{"rows": above, "cols": other}, {"rows": below, "cols": other}]
        if offset:
            peers.append({"cols": other})
    for peer in peers:
        pl.semaphore_signal(barrier, inc=1, device_id=peer, device_id_type=pl.DeviceIdType.MESH)
    pl.semaphore_wait(barrier, len(peers))
    send = Sender(send_sems, recv_sems)

    ham_first = send(ham_ref, ham_v.at[col], side)
    ham_second = send(ham_ref, ham_v.at[col], cross)

    def land(piece, k, part=None):
        size = half if part is None else half // 2
        start = half * space + (0 if part is None else part * size)
        return land_v.at[
            piece // 2,
            piece % 2,
            pl.ds(pl.multiple_of(start, size), size),
            pl.ds(pl.multiple_of(chunk * k, chunk), chunk),
        ]

    order_of_pieces = (0, 2, 1, 3)
    pieces = {}
    for piece in order_of_pieces:
        panel = (1, 2, 1, 0)[piece]
        source = root_ref.at[
            pl.ds(pl.multiple_of(half * space, half), half),
            pl.ds(pl.multiple_of(panel * slab + chunk * col, chunk), chunk),
        ]
        pieces[piece] = send(source, land(piece, col), up if piece < 2 else down)

    zero = jnp.zeros(ortho_v.shape[3:], F32)
    for part in range(2):
        ortho_v[0, 2, part] = zero
        ortho_v[2, 0, part] = zero

    pattern = pattern_ref[...].astype(F32).astype(BF16)
    blocks_all = pattern.shape[0]

    def pick(rows, block_of):
        wanted = block_of(lax.broadcasted_iota(jnp.int32, (rows, blocks_all), 0))
        here = lax.broadcasted_iota(jnp.int32, (rows, blocks_all), 1)
        return dot(jnp.where(wanted == here, 1.0, 0.0).astype(BF16), pattern).astype(BF16)

    def spread(values, wanted):
        here = lax.broadcasted_iota(jnp.int32, wanted.shape, 0)
        return dot(values, jnp.where(wanted == here, 1.0, 0.0).astype(BF16))

    base = row * slab_blocks
    strip_rows = pick(
        cols * own,
        lambda i: base + ((i // own) * 2 + space) * own_blocks + (i % own) // BLK,
    )
    lane = lax.broadcasted_iota(jnp.int32, (3 * slab_blocks, 3 * chunk), 1)
    chip_mask = spread(
        strip_rows, (lane // chunk) * slab_blocks + col * groups + (lane % chunk) // BLK
    )
    for i in range(cols):
        mask_a[i] = chip_mask[i * own : (i + 1) * own]
    own_rows = pick(own, lambda i: base + (col * 2 + space) * own_blocks + i // BLK)
    lane = lax.broadcasted_iota(jnp.int32, (3 * slab_blocks, window), 1)
    mask_b[...] = spread(own_rows, lane // BLK)

    load_root.wait()
    for i in range(cols):
        start = pl.multiple_of((i * 2 + space) * own, own)
        upper, lower = split(root_v[pl.ds(start, own), :])
        left_s[0, i * own : (i + 1) * own] = upper
        left_s[1, i * own : (i + 1) * own] = lower
    for b in range(3):
        wide_hi[1, b], wide_lo[1, b] = split(root_v[:, b * slab : (b + 1) * slab])
        start = pl.multiple_of(b * slab + chunk * col, chunk)
        upper, lower = split(root_v[:, pl.ds(start, chunk)])
        near_hi[1, :, b * chunk : (b + 1) * chunk] = upper
        near_lo[1, :, b * chunk : (b + 1) * chunk] = lower

    relayed = {}
    gathers = {}

    def arrive(piece):
        pieces[piece].wait_recv()
        relayed[piece] = send(land(piece, col), land(piece, col), mate)

    def offer(piece):
        gathers[piece] = [
            send(land(piece, col), land(piece, col), side),
            send(land(piece, col), land(piece, col), cross),
        ]

    def half_rows(k, part):
        return ham_v.at[k, pl.ds(part * (own // 2), own // 2), :]

    arrive(0)
    arrive(2)
    ham_first.wait_recv()
    ham_half_a = send(half_rows(first, 1), half_rows(first, 1), cross)
    ham_second.wait_recv()
    ham_half_b = send(half_rows(second, 0), half_rows(second, 0), side)
    offer(0)
    offer(2)
    arrive(1)
    arrive(3)
    offer(1)
    offer(3)
    for piece in order_of_pieces:
        relayed[piece].wait_recv()
        upper, lower = split(land_v[piece // 2, piece % 2, :, lanes])
        side_of = 0 if piece < 2 else 2
        place = (0, 1, 1, 0)[piece]
        near_hi[side_of, :, place * chunk : (place + 1) * chunk] = upper
        near_lo[side_of, :, place * chunk : (place + 1) * chunk] = lower

    load_ham.wait()
    strips = (col, first, second, third)
    half_up, half_down, half_mate = [], [], []
    for i, strip in enumerate(strips):
        if i == 3:
            ham_half_a.wait_recv()
            ham_half_b.wait_recv()
        stacked = stack(ham_v[strip])
        terms = []
        for a in range(3):
            width = 3 * chunk if a == 1 else 2 * chunk
            terms.append(
                product(
                    stacked[:, a * slab : (a + 1) * slab],
                    (near_hi[a, :, :width], near_lo[a, :, :width]),
                )
            )
        done = mask_a[strip] * combine(*terms, chunk)
        for b in range(3):
            half_v[1, b, strip, space] = done[:, b * chunk : (b + 1) * chunk]
        half_up.append(
            send(
                half_v.at[1, pl.ds(1, 2), strip, space],
                half_v.at[0, pl.ds(0, 2), strip, space],
                up,
            )
        )
        half_down.append(
            send(
                half_v.at[1, pl.ds(0, 2), strip, space],
                half_v.at[2, pl.ds(1, 2), strip, space],
                down,
            )
        )
        half_mate.append(
            send(half_v.at[1, :, strip, space], half_v.at[1, :, strip, space], mate)
        )

    def window_block(ref, a):
        picked = {0: (0, 1), 1: (0, 1, 2), 2: (1, 2)}[a]
        return split(
            jnp.concatenate([ref[a, b].reshape(slab, chunk) for b in picked], axis=1)
        )

    def left_block(a):
        return left_s[:, :, a * slab : (a + 1) * slab].reshape(2 * half, slab)

    for copy in half_mate:
        copy.wait_recv()
    acc_v[...] = product(left_block(1), window_block(half_v, 1))
    relays = []
    mates = []
    for i, piece in enumerate(order_of_pieces):
        gathers[piece][0].wait_recv()
        relays.append(send(land(piece, first, 1), land(piece, first, 1), cross))
        mates.append(send(land(piece, first), land(piece, first), mate))
        gathers[piece][1].wait_recv()
        relays.append(send(land(piece, second, 0), land(piece, second, 0), side))
        mates.append(send(land(piece, second), land(piece, second), mate))
        half_up[i].wait_recv()
        region = half_v.at[0, pl.ds(0, 2), strips[i], space]
        half_mate.append(send(region, region, mate))
        half_down[i].wait_recv()
        region = half_v.at[2, pl.ds(1, 2), strips[i], space]
        half_mate.append(send(region, region, mate))
    for copy in half_mate[cols:]:
        copy.wait_recv()

    done = combine(
        product(left_block(0), window_block(half_v, 0)),
        acc_v[...],
        product(left_block(2), window_block(half_v, 2)),
        chunk,
    )
    for b in range(3):
        masked = mask_a[:, :, b * chunk : (b + 1) * chunk].reshape(half, chunk)
        masked = masked * done[:, b * chunk : (b + 1) * chunk]
        ortho_v[1, b, space, :, col] = masked.reshape(half // BLK, BLK, chunk)

    spans = {0: (0, 2), 1: (0, 3), 2: (1, 2)}

    def region(a, k, part=None, span=None):
        size = half // BLK if part is None else half // BLK // 2
        start = 0 if part is None else part * size
        return ortho_v.at[a, pl.ds(*(span or spans[a])), space, pl.ds(start, size), k]

    def pass_on(a, k, part, device):
        return send(region(a, k, part), region(a, k, part), device)

    def to_rows(k, part):
        return (
            send(region(1, k, part, (1, 2)), region(0, k, part), up),
            send(region(1, k, part, (0, 2)), region(2, k, part), down),
        )

    pending = []
    own_rows_out = to_rows(col, None)
    own_first = pass_on(1, col, None, side)
    own_second = pass_on(1, col, None, cross)
    pending.append(pass_on(1, col, None, mate))
    for copy in relays:
        copy.wait_recv()
    for piece in order_of_pieces:
        mates.append(send(land(piece, third), land(piece, third), mate))
    for copy in mates:
        copy.wait_recv()
    for piece in order_of_pieces:
        a = 0 if piece < 2 else 2
        b = (0, 1, 2, 1)[piece]
        wide_hi[a, b], wide_lo[a, b] = split(land_v[piece // 2, piece % 2])

    own_first.wait_recv()
    diagonal_a = pass_on(1, first, 1, cross)
    first_rows = to_rows(first, 0)
    pending.append(pass_on(1, first, None, mate))
    own_second.wait_recv()
    diagonal_b = pass_on(1, second, 0, side)
    second_rows = to_rows(second, 1)
    pending.append(pass_on(1, second, None, mate))
    hops = []
    for a, copy in ((0, own_rows_out[0]), (2, own_rows_out[1])):
        copy.wait_recv()
        hops.append((a, first, 1, pass_on(a, col, 1, side)))
        hops.append((a, second, 0, pass_on(a, col, 0, cross)))
        pending.append(pass_on(a, col, None, mate))
    diagonal_a.wait_recv()
    diagonal_b.wait_recv()
    pending.append(pass_on(1, third, None, mate))
    for a, copy in ((0, first_rows[0]), (2, first_rows[1])):
        copy.wait_recv()
        hops.append((a, third, 0, pass_on(a, first, 0, cross)))
        pending.append(pass_on(a, first, 0, mate))
    for a, copy in ((0, second_rows[0]), (2, second_rows[1])):
        copy.wait_recv()
        hops.append((a, third, 1, pass_on(a, second, 1, side)))
        pending.append(pass_on(a, second, 1, mate))
    for a, k, part, copy in hops:
        copy.wait_recv()
        pending.append(pass_on(a, k, part, mate))
    for copy in pending:
        copy.wait_recv()

    lane_group = lax.broadcasted_iota(jnp.int32, (BLK, chunk), 1) // BLK

    def turn(value, steps):
        steps = jnp.full((BLK, chunk), steps, jnp.int32)
        step = 1
        while step < groups:
            moved = pltpu.roll(value, step * BLK, 1)
            value = jnp.where(steps & step == step, moved, value)
            step *= 2
        return value

    def solve(g, carry):
        live = count_ref[g]

        def assemble(i, inner):
            block = pos_ref[g, i]
            a = lax.div(block, slab_blocks)
            within = lax.rem(block, slab_blocks)
            owner = lax.div(within, own_blocks)
            core = lax.rem(owner, 2)
            place = lax.div(owner, 2) * own_blocks + lax.rem(within, own_blocks)
            for t in range(maxb // groups):
                tile = jnp.zeros((BLK, chunk), F32)
                for e in range(groups):
                    other = pos_ref[g, t * groups + e]
                    b = lax.div(other, slab_blocks)
                    inside = lax.rem(other, slab_blocks)
                    value = ortho_v[a, b, core, place, lax.div(inside, groups)]
                    value = turn(value, lax.rem(e + groups - lax.rem(inside, groups), groups))
                    tile = jnp.where(lane_group == e, value, tile)
                sub_v[pl.ds(pl.multiple_of(i * BLK, BLK), BLK), t * chunk : (t + 1) * chunk] = tile
            return inner

        lax.fori_loop(0, maxb, assemble, 0)
        position = [lax.broadcasted_iota(jnp.int32, (order, order), d) for d in range(2)]
        assembled = jnp.where(jnp.maximum(*position) < live * BLK, sub_v[...], 0.0)
        symmetric = 0.5 * (assembled + assembled.T)
        total = jnp.sum(jnp.sum(symmetric * symmetric, axis=1, keepdims=True), axis=0, keepdims=True)
        live_order = jnp.full((1, 1), live * BLK, jnp.int32).astype(F32)
        iterate = symmetric * (jnp.sqrt(live_order) / (2.0 * jnp.sqrt(total + 1e-06)))
        parts = split(iterate)
        square = split(product(jnp.concatenate(parts, axis=0), parts))

        def times_square(value):
            return product(stack(value), square)

        home = iterate[:BLK]
        home = 1.5 * home - 0.5 * times_square(home)
        cube = times_square(home)
        cube = 1.5 * cube - 0.5 * times_square(cube)
        cube = 1.5 * cube - 0.5 * times_square(cube)
        home = 1.5 * home - 0.5 * cube
        diagonal = lax.broadcasted_iota(jnp.int32, (BLK, order), 0) == lax.broadcasted_iota(
            jnp.int32, (BLK, order), 1
        )
        home = 0.5 * (jnp.where(diagonal, 1.0, 0.0) - home)
        tiles = [jnp.zeros((BLK, chunk), F32) for _ in range(window // chunk)]
        for p in range(maxb):
            other = pos_ref[g, p]
            sub = lax.rem(other, groups)
            t = p // groups
            value = home[:, t * chunk : (t + 1) * chunk]
            value = turn(value, lax.rem(sub + groups - p % groups, groups))
            value = jnp.where(lane_group == jnp.full((BLK, chunk), sub, jnp.int32), value, 0.0)
            place = jnp.full((BLK, chunk), lax.div(other, groups), jnp.int32)
            value = jnp.where(jnp.full((BLK, chunk), live, jnp.int32) > p, value, 0.0)
            for m in range(len(tiles)):
                tiles[m] += jnp.where(place == m, value, 0.0)
        for m, tile in enumerate(tiles):
            band_v[g, :, m * chunk : (m + 1) * chunk] = tile
        return carry

    lax.fori_loop(0, own_blocks, solve, 0)

    stacked = stack(band_v[...].reshape(own, window))
    for b in range(3):
        total = None
        for a in (0, 1, 2):
            if abs(a - b) > 1:
                continue
            term = product(stacked[:, a * slab : (a + 1) * slab], (wide_hi[a, b], wide_lo[a, b]))
            total = term if total is None else total + term
        rows_v[b] = mask_b[:, b * slab : (b + 1) * slab] * total

    def lanes_of(k):
        return pl.ds(pl.multiple_of(chunk * k, chunk), chunk)

    back = []
    for offset in (2, 1, 3, 0):
        target = lax.rem(col + offset, cols)
        origin = lax.rem(col + cols - offset, cols)
        for a, span, device in ((0, (1, 2), above), (2, (0, 2), below)):
            copy = send(
                rows_v.at[pl.ds(*span), :, lanes_of(target)],
                back_v.at[a, pl.ds(*spans[a]), col, space],
                {"rows": device, "cols": target},
            )
            back.append((a, origin, copy))
    for offset in (2, 1, 3):
        target = lax.rem(col + offset, cols)
        origin = lax.rem(col + cols - offset, cols)
        copy = send(
            rows_v.at[:, :, lanes_of(target)],
            back_v.at[1, :, col, space],
            {"cols": target},
        )
        back.append((1, origin, copy))
    back_mate = [send(rows_v.at[:, :, lanes], back_v.at[1, :, col, space], mate)]
    back_v[1, :, col, space] = rows_v[:, :, lanes]
    for a, origin, copy in sorted(back, key=lambda item: item[0] != 1):
        copy.wait_recv()
        piece = back_v.at[a, pl.ds(*spans[a]), origin, space]
        back_mate.append(send(piece, piece, mate))
        if len(back_mate) == cols:
            for other in back_mate:
                other.wait_recv()
            acc_v[...] = product(left_block(1), window_block(back_v, 1))
    for other in back_mate[cols:]:
        other.wait_recv()
    done = combine(
        product(left_block(0), window_block(back_v, 0)),
        acc_v[...],
        product(left_block(2), window_block(back_v, 2)),
        chunk,
    )
    for b in range(3):
        masked = mask_a[:, :, b * chunk : (b + 1) * chunk].reshape(half, chunk)
        piece = masked * done[:, b * chunk : (b + 1) * chunk]
        strip_v[:, b] = piece.reshape(cols, own, chunk)
    outs = []
    for offset in (2, 1, 3):
        target = lax.rem(col + offset, cols)
        outs.append(send(strip_v.at[target], final_v.at[col], {"cols": target}))
    final_v[col] = strip_v[col]
    for copy in outs:
        copy.wait_recv()
    total = jnp.zeros((own, chunk), F32)
    for b in range(3):
        for k in range(cols):
            value = final_v[k, b]
            total = total + value
            density_ref[:, b * slab + k * chunk : b * slab + (k + 1) * chunk] = value
    charges_ref[...] = jnp.sum(total.T, axis=0, keepdims=True)
    send.finish()


def shards(hamiltonian, correlation_root, pattern, sub_blocks, sub_count):
    slab, window = correlation_root.shape
    own = hamiltonian.shape[0]
    cols = lax.axis_size("cols")
    chunk = slab // cols
    half = slab // 2
    own_blocks, maxb = sub_blocks.shape
    order = maxb * BLK
    vmem = functools.partial(pltpu.VMEM)
    density, charges = pl.pallas_call(
        kernel,
        out_shape=[
            jax.ShapeDtypeStruct((own, window), F32),
            jax.ShapeDtypeStruct((1, own), F32),
        ],
        in_specs=[
            pl.BlockSpec(memory_space=pltpu.SMEM),
            pl.BlockSpec(memory_space=pltpu.SMEM),
            pl.BlockSpec(memory_space=pl.ANY),
            pl.BlockSpec(memory_space=pl.ANY),
            pl.BlockSpec(memory_space=pltpu.VMEM),
        ],
        out_specs=[pl.BlockSpec(memory_space=pltpu.VMEM)] * 2,
        scratch_shapes=[
            vmem((slab, window), F32),
            vmem((2, half, window), BF16),
            vmem((cols, own, window), F32),
            vmem((2, 2, slab, slab), F32),
            vmem((3, 3, slab, slab), BF16),
            vmem((3, 3, slab, slab), BF16),
            vmem((3, slab, 3 * chunk), BF16),
            vmem((3, slab, 3 * chunk), BF16),
            vmem((cols, own, 3 * chunk), F32),
            vmem((own, window), F32),
            vmem((3, 3, cols, 2, own, chunk), F32),
            vmem((3, 3, cols, 2, own, chunk), F32),
            vmem((3, 3, 2, half // BLK, cols, BLK, chunk), F32),
            vmem((half, 3 * chunk), F32),
            vmem((order, order), F32),
            vmem((own_blocks, BLK, window), F32),
            vmem((3, own, slab), F32),
            vmem((cols, 3, own, chunk), F32),
            vmem((cols, 3, own, chunk), F32),
            pltpu.SemaphoreType.DMA((2,)),
            pltpu.SemaphoreType.DMA((160,)),
            pltpu.SemaphoreType.DMA((160,)),
        ],
        compiler_params=pltpu.CompilerParams(
            collective_id=1, has_side_effects=True, vmem_limit_bytes=60 * 2**20
        ),
    )(sub_blocks, sub_count, hamiltonian, correlation_root, pattern)
    return density, charges.reshape(own)


def solution(mesh):
    return jax.shard_map(
        shards,
        mesh=mesh,
        in_specs=(
            P(("rows", "cols", "space"), None),
            P("rows", None),
            P(),
            P(("rows", "cols", "space"), None),
            P(("rows", "cols", "space")),
        ),
        out_specs=(P(("rows", "cols", "space"), None), P(("rows", "cols", "space"))),
        check_vma=False,
    )
```

time: 161 us -> 116 us (0.72)
  Pallas kernels: 124 us -> 111 us
  local copies, waits for them, and re-layouts: 14.4 us -> 4.32 us
  waiting for transfers between devices: 8.01 us -> 0 us
  matrix products: 6.8 us -> 0 us
  other arithmetic: 3.81 us -> 0 us
  starting transfers between devices: 3.45 us -> 0 us
    pallas_call x6 -> x1, Pallas kernels: 124 us -> 111 us  [shards(): pl.pallas_call(kernel, out_shape=[jax.ShapeDtypeStruct((own, window), F32...]
    all_to_all x1 -> x0, waiting for transfers between devices: 8.01 us -> none  [shards(): lax.all_to_all(density.transpose(2, 3, 0, 1), GROUP, 0, 0, tiled=False)]
    dot_general x4 -> x0, matrix products: 6.8 us -> none  [multiply_nt(): lax.dot_general(leftside, rightside, (((1,), (1,)), ((), ())), precision=...]
    unnamed x16 -> x3, local copies, waits for them, and re-layouts: 10.8 us -> 4.32 us
    all_to_all x1 -> x0, starting transfers between devices: 3.45 us -> none  [shards(): lax.all_to_all(density.transpose(2, 3, 0, 1), GROUP, 0, 0, tiled=False)]
  transfers between devices with their start and end apart: 1 -> 0, of which waited for: 1 -> 0; matrix products, arithmetic and copies ran while one was open for 0% -> 0% of each run, Pallas kernels for 0% -> 0%
where the time goes in v1:
time: 116 us
  Pallas kernels  111 us (96%)
  local copies, waits for them, and re-layouts  4.32 us (4%)
    pallas_call x1, Pallas kernels, shards(): pl.pallas_call(kernel, out_shape=[jax.ShapeDtypeStruct((own, window), F32...  111 us
    unnamed x3, local copies, waits for them, and re-layouts  4.32 us

profile of v1, /device:TPU:0, one launch (start us, length us, event | category | flops | bytes accessed | tf_op | source)
XLA Modules:
  0.0 115.7 jit_solution(15284437627377247850)
XLA Ops:
  0.6 1.4 %copy.7.pattern_ref = s32[64,48]{1,0:T(8,128)} copy(s32[64,48]{0,1:T(8,128)} %param.7) | data formatting | bytes 24576 | tf_op args[2]
  2.1 110.7 %shard_map.68 = (f32[64,1536]{1,0:T(8,128)}, f32[1,64]{1,0:T(1,128)}) custom-call(s32[2,16]{1,0:T(2,128)} %pos_ref.1, s32[2]{0:T(128)} %count_ref.1, f32[64,1536]{1,0:T(8,128)} %ham_ref.1, f32[512,1536]{1,0:T(8,128)} %root_ref.1, s32[64,48]{1,0:T(8,128)} %copy.7.pattern_ref), custom_call_target="tpu_custom_call" | custom-call | tf_op jit(solution)/shard_map/pallas_call | solution.py:543
  112.8 1.8 %copy.10 = f32[64,1536]{1,0:T(8,128)} copy(f32[64,1536]{1,0:T(8,128)} %get-tuple-element.8) | data formatting | bytes 786432
  114.6 1.1 copy.11

commit v2 on v1

--- a/solution.py
+++ b/solution.py
@@ -90,7 +90,7 @@
     ortho_v,
     acc_v,
     sub_v,
-    band_v,
+    turns_v,
     rows_v,
     strip_v,
     final_v,
@@ -168,12 +168,15 @@
         ortho_v[2, 0, part] = zero
 
     pattern = pattern_ref[...].astype(F32).astype(BF16)
-    blocks_all = pattern.shape[0]
+    blocks_all = pattern.shape[1]
 
     def pick(rows, block_of):
         wanted = block_of(lax.broadcasted_iota(jnp.int32, (rows, blocks_all), 0))
         here = lax.broadcasted_iota(jnp.int32, (rows, blocks_all), 1)
-        return dot(jnp.where(wanted == here, 1.0, 0.0).astype(BF16), pattern).astype(BF16)
+        chosen = jnp.where(wanted == here, 1.0, 0.0).astype(BF16)
+        return lax.dot_general(
+            chosen, pattern, (((1,), (1,)), ((), ())), preferred_element_type=F32
+        ).astype(BF16)
 
     def spread(values, wanted):
         here = lax.broadcasted_iota(jnp.int32, wanted.shape, 0)
@@ -385,19 +388,19 @@
     for copy in pending:
         copy.wait_recv()
 
-    lane_group = lax.broadcasted_iota(jnp.int32, (BLK, chunk), 1) // BLK
-
-    def turn(value, steps):
-        steps = jnp.full((BLK, chunk), steps, jnp.int32)
-        step = 1
-        while step < groups:
-            moved = pltpu.roll(value, step * BLK, 1)
-            value = jnp.where(steps & step == step, moved, value)
-            step *= 2
-        return value
-
-    def solve(g, carry):
+    lane_group = lax.broadcasted_iota(jnp.int32, (8, chunk), 1) // BLK
+
+    def solve(g):
         live = count_ref[g]
+
+        for p in range(maxb):
+            sub = lax.rem(pos_ref[g, p], groups)
+            steps = lax.rem(p + groups - sub, groups)
+            turns_v[p] = jnp.where(
+                lane_group == jnp.full(lane_group.shape, sub, jnp.int32),
+                jnp.full(lane_group.shape, steps, jnp.int32),
+                -1,
+            )
 
         def assemble(i, inner):
             block = pos_ref[g, i]
@@ -407,14 +410,19 @@
             core = lax.rem(owner, 2)
             place = lax.div(owner, 2) * own_blocks + lax.rem(within, own_blocks)
             for t in range(maxb // groups):
-                tile = jnp.zeros((BLK, chunk), F32)
+                sorted_by = [jnp.zeros((BLK, chunk), F32)] * groups
                 for e in range(groups):
-                    other = pos_ref[g, t * groups + e]
+                    p = t * groups + e
+                    other = pos_ref[g, p]
                     b = lax.div(other, slab_blocks)
-                    inside = lax.rem(other, slab_blocks)
-                    value = ortho_v[a, b, core, place, lax.div(inside, groups)]
-                    value = turn(value, lax.rem(e + groups - lax.rem(inside, groups), groups))
-                    tile = jnp.where(lane_group == e, value, tile)
+                    k = lax.div(lax.rem(other, slab_blocks), groups)
+                    value = ortho_v[a, b, core, place, k]
+                    needed = jnp.tile(turns_v[p], (BLK // 8, 1))
+                    for steps in range(groups):
+                        sorted_by[steps] = jnp.where(needed == steps, value, sorted_by[steps])
+                tile = sorted_by[0]
+                for steps in range(1, groups):
+                    tile = tile + pltpu.roll(sorted_by[steps], steps * BLK, 1)
                 sub_v[pl.ds(pl.multiple_of(i * BLK, BLK), BLK), t * chunk : (t + 1) * chunk] = tile
             return inner
 
@@ -426,7 +434,7 @@
         live_order = jnp.full((1, 1), live * BLK, jnp.int32).astype(F32)
         iterate = symmetric * (jnp.sqrt(live_order) / (2.0 * jnp.sqrt(total + 1e-06)))
         parts = split(iterate)
-        square = split(product(jnp.concatenate(parts, axis=0), parts))
+        square = split(dot(parts[0], parts[0]) + dot(parts[0], parts[1]) + dot(parts[1], parts[0]))
 
         def times_square(value):
             return product(stack(value), square)
@@ -442,67 +450,83 @@
         )
         home = 0.5 * (jnp.where(diagonal, 1.0, 0.0) - home)
         tiles = [jnp.zeros((BLK, chunk), F32) for _ in range(window // chunk)]
+        turned = [
+            [home[:, t * chunk : (t + 1) * chunk]]
+            + [
+                pltpu.roll(home[:, t * chunk : (t + 1) * chunk], steps * BLK, 1)
+                for steps in range(1, groups)
+            ]
+            for t in range(maxb // groups)
+        ]
         for p in range(maxb):
             other = pos_ref[g, p]
             sub = lax.rem(other, groups)
-            t = p // groups
-            value = home[:, t * chunk : (t + 1) * chunk]
-            value = turn(value, lax.rem(sub + groups - p % groups, groups))
-            value = jnp.where(lane_group == jnp.full((BLK, chunk), sub, jnp.int32), value, 0.0)
-            place = jnp.full((BLK, chunk), lax.div(other, groups), jnp.int32)
-            value = jnp.where(jnp.full((BLK, chunk), live, jnp.int32) > p, value, 0.0)
+            here = (lane_group == jnp.full(lane_group.shape, sub, jnp.int32)) & (
+                jnp.full(lane_group.shape, live, jnp.int32) > p
+            )
+            place = jnp.where(
+                here, jnp.full(lane_group.shape, lax.div(other, groups), jnp.int32), -1
+            )
+            place = jnp.tile(place, (BLK // 8, 1))
+            ways = turned[p // groups]
+            wide = jnp.tile(lane_group, (BLK // 8, 1))
+            value = ways[(groups - p) % groups]
+            for target in range(1, groups):
+                value = jnp.where(wide == target, ways[(target + groups - p) % groups], value)
             for m in range(len(tiles)):
-                tiles[m] += jnp.where(place == m, value, 0.0)
-        for m, tile in enumerate(tiles):
-            band_v[g, :, m * chunk : (m + 1) * chunk] = tile
-        return carry
-
-    lax.fori_loop(0, own_blocks, solve, 0)
-
-    stacked = stack(band_v[...].reshape(own, window))
-    for b in range(3):
-        total = None
-        for a in (0, 1, 2):
-            if abs(a - b) > 1:
-                continue
-            term = product(stacked[:, a * slab : (a + 1) * slab], (wide_hi[a, b], wide_lo[a, b]))
-            total = term if total is None else total + term
-        rows_v[b] = mask_b[:, b * slab : (b + 1) * slab] * total
+                tiles[m] = jnp.where(place == m, value, tiles[m])
+        return jnp.concatenate(tiles, axis=1)
 
     def lanes_of(k):
         return pl.ds(pl.multiple_of(chunk * k, chunk), chunk)
 
-    back = []
-    for offset in (2, 1, 3, 0):
-        target = lax.rem(col + offset, cols)
-        origin = lax.rem(col + cols - offset, cols)
-        for a, span, device in ((0, (1, 2), above), (2, (0, 2), below)):
+    back, back_mate = [], []
+    for g in range(own_blocks):
+        stacked = stack(solve(g))
+        these = slice(g * BLK, (g + 1) * BLK)
+        for b in range(3):
+            total = None
+            for a in (0, 1, 2):
+                if abs(a - b) > 1:
+                    continue
+                term = product(
+                    stacked[:, a * slab : (a + 1) * slab], (wide_hi[a, b], wide_lo[a, b])
+                )
+                total = term if total is None else total + term
+            rows_v[b, these] = mask_b[these, b * slab : (b + 1) * slab] * total
+        these = pl.ds(g * BLK, BLK)
+        for offset in (2, 1, 3, 0):
+            target = lax.rem(col + offset, cols)
+            origin = lax.rem(col + cols - offset, cols)
+            for a, span, device in ((0, (1, 2), above), (2, (0, 2), below)):
+                copy = send(
+                    rows_v.at[pl.ds(*span), these, lanes_of(target)],
+                    back_v.at[a, pl.ds(*spans[a]), col, space, these],
+                    {"rows": device, "cols": target},
+                )
+                back.append((a, g, origin, copy))
+        for offset in (2, 1, 3):
+            target = lax.rem(col + offset, cols)
+            origin = lax.rem(col + cols - offset, cols)
             copy = send(
-                rows_v.at[pl.ds(*span), :, lanes_of(target)],
-                back_v.at[a, pl.ds(*spans[a]), col, space],
-                {"rows": device, "cols": target},
+                rows_v.at[:, these, lanes_of(target)],
+                back_v.at[1, :, col, space, these],
+                {"cols": target},
             )
-            back.append((a, origin, copy))
-    for offset in (2, 1, 3):
-        target = lax.rem(col + offset, cols)
-        origin = lax.rem(col + cols - offset, cols)
-        copy = send(
-            rows_v.at[:, :, lanes_of(target)],
-            back_v.at[1, :, col, space],
-            {"cols": target},
-        )
-        back.append((1, origin, copy))
-    back_mate = [send(rows_v.at[:, :, lanes], back_v.at[1, :, col, space], mate)]
+            back.append((1, g, origin, copy))
+        back_mate.append(
+            send(rows_v.at[:, these, lanes], back_v.at[1, :, col, space, these], mate)
+        )
     back_v[1, :, col, space] = rows_v[:, :, lanes]
-    for a, origin, copy in sorted(back, key=lambda item: item[0] != 1):
-        copy.wait_recv()
-        piece = back_v.at[a, pl.ds(*spans[a]), origin, space]
+    for a, g, origin, copy in sorted(back, key=lambda item: (item[0] != 1, item[1])):
+        copy.wait_recv()
+        piece = back_v.at[a, pl.ds(*spans[a]), origin, space, pl.ds(g * BLK, BLK)]
         back_mate.append(send(piece, piece, mate))
-        if len(back_mate) == cols:
+        if len(back_mate) == own_blocks * cols:
             for other in back_mate:
                 other.wait_recv()
             acc_v[...] = product(left_block(1), window_block(back_v, 1))
-    for other in back_mate[cols:]:
+    for other in back_mate[own_blocks * cols :]:
         other.wait_recv()
     done = combine(
         product(left_block(0), window_block(back_v, 0)),
@@ -527,8 +551,26 @@
             value = final_v[k, b]
             total = total + value
             density_ref[:, b * slab + k * chunk : b * slab + (k + 1) * chunk] = value
-    charges_ref[...] = jnp.sum(total.T, axis=0, keepdims=True)
+    charges_ref[...] = jnp.sum(total.T, axis=0)
     send.finish()
+
+
+def place_kernel(density_ref, charges_ref, density_out, charges_out, density_v, charges_v, sems):
+    inward = [
+        pltpu.make_async_copy(density_ref, density_v, sems.at[0]),
+        pltpu.make_async_copy(charges_ref, charges_v, sems.at[1]),
+    ]
+    outward = [
+        pltpu.make_async_copy(density_v, density_out, sems.at[2]),
+        pltpu.make_async_copy(charges_v, charges_out, sems.at[3]),
+    ]
+    for copy in inward:
+        copy.start()
+    for copy, then in zip(inward, outward):
+        copy.wait()
+        then.start()
+    for copy in outward:
+        copy.wait()
 
 
 def shards(hamiltonian, correlation_root, pattern, sub_blocks, sub_count):
@@ -544,13 +586,13 @@
         kernel,
         out_shape=[
             jax.ShapeDtypeStruct((own, window), F32),
-            jax.ShapeDtypeStruct((1, own), F32),
+            jax.ShapeDtypeStruct((own,), F32),
         ],
         in_specs=[
             pl.BlockSpec(memory_space=pltpu.SMEM),
             pl.BlockSpec(memory_space=pltpu.SMEM),
-            pl.BlockSpec(memory_space=pl.ANY),
-            pl.BlockSpec(memory_space=pl.ANY),
+            pl.BlockSpec(memory_space=pltpu.HBM),
+            pl.BlockSpec(memory_space=pltpu.HBM),
             pl.BlockSpec(memory_space=pltpu.VMEM),
         ],
         out_specs=[pl.BlockSpec(memory_space=pltpu.VMEM)] * 2,
@@ -570,19 +612,33 @@
             vmem((3, 3, 2, half // BLK, cols, BLK, chunk), F32),
             vmem((half, 3 * chunk), F32),
             vmem((order, order), F32),
-            vmem((own_blocks, BLK, window), F32),
+            vmem((maxb, 8, chunk), jnp.int32),
             vmem((3, own, slab), F32),
             vmem((cols, 3, own, chunk), F32),
             vmem((cols, 3, own, chunk), F32),
             pltpu.SemaphoreType.DMA((2,)),
-            pltpu.SemaphoreType.DMA((160,)),
-            pltpu.SemaphoreType.DMA((160,)),
+            pltpu.SemaphoreType.DMA((200,)),
+            pltpu.SemaphoreType.DMA((200,)),
         ],
         compiler_params=pltpu.CompilerParams(
-            collective_id=1, has_side_effects=True, vmem_limit_bytes=60 * 2**20
+            collective_id=1, has_side_effects=True, vmem_limit_bytes=62 * 2**20
         ),
-    )(sub_blocks, sub_count, hamiltonian, correlation_root, pattern)
-    return density, charges.reshape(own)
+    )(sub_blocks, sub_count, hamiltonian, correlation_root, pattern.T)
+    return pl.pallas_call(
+        place_kernel,
+        out_shape=[
+            jax.ShapeDtypeStruct((own, window), F32),
+            jax.ShapeDtypeStruct((own,), F32),
+        ],
+        in_specs=[pl.BlockSpec(memory_space=pltpu.HBM)] * 2,
+        out_specs=[pl.BlockSpec(memory_space=pltpu.HBM)] * 2,
+        scratch_shapes=[
+            pltpu.VMEM((own, window), F32),
+            pltpu.VMEM((own,), F32),
+            pltpu.SemaphoreType.DMA((4,)),
+        ],
+        compiler_params=pltpu.CompilerParams(vmem_limit_bytes=62 * 2**20),
+    )(density, charges)
 
 
 def solution(mesh):

time: 116 us -> 108 us (0.931)
  local copies, waits for them, and re-layouts: 4.32 us -> 0 us
  Pallas kernels: 111 us -> 107 us
    pallas_call x1, Pallas kernels: 111 us -> 105 us  [shards(): pl.pallas_call(kernel, out_shape=[jax.ShapeDtypeStruct((own, window), F32...]
    unnamed x3 -> x0, local copies, waits for them, and re-layouts: 4.32 us -> none
    pallas_call x0 -> x1, Pallas kernels: none -> 1.78 us  [shards(): pl.pallas_call(place_kernel, out_shape=[jax.ShapeDtypeStruct((own, window...]
where the time goes in v2:
time: 108 us; the launch traced here: 107 us
  Pallas kernels  107 us (99%)
    pallas_call x1, Pallas kernels, shards(): pl.pallas_call(kernel, out_shape=[jax.ShapeDtypeStruct((own, window), F32...  105 us

profile of v2, /device:TPU:0, one launch (start us, length us, event | category | flops | bytes accessed | tf_op | source)
XLA Modules:
  0.0 107.3 jit_solution(5707013347149018447)
XLA Ops:
  0.6 104.8 %shard_map.68 = (f32[64,1536]{1,0:T(8,128)}, f32[64]{0:T(128)}) custom-call(s32[2,16]{1,0:T(2,128)} %pos_ref.1, s32[2]{0:T(128)} %count_ref.1, f32[64,1536]{1,0:T(8,128)} %ham_ref.1, f32[512,1536]{1,0:T(8,128)} %root_ref.1, s32[48,64]{1,0:T(8,128)} %bitcast.1), custom_call_target="tpu_custom_call" | custom-call | tf_op jit(solution)/shard_map/pallas_call | solution.py:585
  105.4 1.8 %shard_map.69 = (f32[64,1536]{1,0:T(8,128)}, f32[64]{0:T(128)}) custom-call(f32[64,1536]{1,0:T(8,128)} %get-tuple-element.4.density_ref, f32[64]{0:T(128)} %get-tuple-element.5.charges_ref), custom_call_target="tpu_custom_call" | custom-call | tf_op jit(solution)/shard_map/pallas_call | solution.py:627

commit v3 on v2

--- a/solution.py
+++ b/solution.py
@@ -68,11 +68,11 @@
 
 
 def kernel(
-    pos_ref,
-    count_ref,
+    pos_in,
+    count_in,
     ham_ref,
     root_ref,
-    pattern_ref,
+    pattern_in,
     density_ref,
     charges_ref,
     root_v,
@@ -94,6 +94,10 @@
     rows_v,
     strip_v,
     final_v,
+    pattern_ref,
+    pos_ref,
+    count_ref,
+    table_s,
     local_sems,
     send_sems,
     recv_sems,
@@ -124,8 +128,15 @@
 
     load_root = pltpu.make_async_copy(root_ref, root_v, local_sems.at[0])
     load_ham = pltpu.make_async_copy(ham_ref, ham_v.at[col], local_sems.at[1])
+    small = [
+        pltpu.make_async_copy(pos_in, pos_ref, local_sems.at[2]),
+        pltpu.make_async_copy(count_in, count_ref, local_sems.at[3]),
+        pltpu.make_async_copy(pattern_in, pattern_ref, local_sems.at[4]),
+    ]
     load_root.start()
     load_ham.start()
+    for copy in small:
+        copy.start()
 
     barrier = pltpu.get_barrier_semaphore()
     peers = [mate]
@@ -167,6 +178,8 @@
         ortho_v[0, 2, part] = zero
         ortho_v[2, 0, part] = zero
 
+    for copy in small:
+        copy.wait()
     pattern = pattern_ref[...].astype(F32).astype(BF16)
     blocks_all = pattern.shape[1]
 
@@ -196,6 +209,17 @@
     own_rows = pick(own, lambda i: base + (col * 2 + space) * own_blocks + i // BLK)
     lane = lax.broadcasted_iota(jnp.int32, (3 * slab_blocks, window), 1)
     mask_b[...] = spread(own_rows, lane // BLK)
+
+    for g in range(own_blocks):
+        for p in range(maxb):
+            block = pos_ref[g, p]
+            within = lax.rem(block, slab_blocks)
+            owner = lax.div(within, own_blocks)
+            table_s[0, g, p] = lax.div(block, slab_blocks)
+            table_s[1, g, p] = lax.rem(owner, 2)
+            table_s[2, g, p] = lax.div(owner, 2) * own_blocks + lax.rem(within, own_blocks)
+            table_s[3, g, p] = lax.div(within, groups)
+            table_s[4, g, p] = lax.rem(within, groups)
 
     load_root.wait()
     for i in range(cols):
@@ -299,18 +323,18 @@
     relays = []
     mates = []
     for i, piece in enumerate(order_of_pieces):
+        half_up[i].wait_recv()
+        region = half_v.at[0, pl.ds(0, 2), strips[i], space]
+        half_mate.append(send(region, region, mate))
+        half_down[i].wait_recv()
+        region = half_v.at[2, pl.ds(1, 2), strips[i], space]
+        half_mate.append(send(region, region, mate))
         gathers[piece][0].wait_recv()
         relays.append(send(land(piece, first, 1), land(piece, first, 1), cross))
         mates.append(send(land(piece, first), land(piece, first), mate))
         gathers[piece][1].wait_recv()
         relays.append(send(land(piece, second, 0), land(piece, second, 0), side))
         mates.append(send(land(piece, second), land(piece, second), mate))
-        half_up[i].wait_recv()
-        region = half_v.at[0, pl.ds(0, 2), strips[i], space]
-        half_mate.append(send(region, region, mate))
-        half_down[i].wait_recv()
-        region = half_v.at[2, pl.ds(1, 2), strips[i], space]
-        half_mate.append(send(region, region, mate))
     for copy in half_mate[cols:]:
         copy.wait_recv()
 
@@ -394,7 +418,7 @@
         live = count_ref[g]
 
         for p in range(maxb):
-            sub = lax.rem(pos_ref[g, p], groups)
+            sub = table_s[4, g, p]
             steps = lax.rem(p + groups - sub, groups)
             turns_v[p] = jnp.where(
                 lane_group == jnp.full(lane_group.shape, sub, jnp.int32),
@@ -403,20 +427,12 @@
             )
 
         def assemble(i, inner):
-            block = pos_ref[g, i]
-            a = lax.div(block, slab_blocks)
-            within = lax.rem(block, slab_blocks)
-            owner = lax.div(within, own_blocks)
-            core = lax.rem(owner, 2)
-            place = lax.div(owner, 2) * own_blocks + lax.rem(within, own_blocks)
+            a, core, place = (table_s[field, g, i] for field in range(3))
             for t in range(maxb // groups):
                 sorted_by = [jnp.zeros((BLK, chunk), F32)] * groups
                 for e in range(groups):
                     p = t * groups + e
-                    other = pos_ref[g, p]
-                    b = lax.div(other, slab_blocks)
-                    k = lax.div(lax.rem(other, slab_blocks), groups)
-                    value = ortho_v[a, b, core, place, k]
+                    value = ortho_v[a, table_s[0, g, p], core, place, table_s[3, g, p]]
                     needed = jnp.tile(turns_v[p], (BLK // 8, 1))
                     for steps in range(groups):
                         sorted_by[steps] = jnp.where(needed == steps, value, sorted_by[steps])
@@ -426,7 +442,7 @@
                 sub_v[pl.ds(pl.multiple_of(i * BLK, BLK), BLK), t * chunk : (t + 1) * chunk] = tile
             return inner
 
-        lax.fori_loop(0, maxb, assemble, 0)
+        lax.fori_loop(0, maxb, assemble, 0, unroll=2)
         position = [lax.broadcasted_iota(jnp.int32, (order, order), d) for d in range(2)]
         assembled = jnp.where(jnp.maximum(*position) < live * BLK, sub_v[...], 0.0)
         symmetric = 0.5 * (assembled + assembled.T)
@@ -480,11 +496,18 @@
     def lanes_of(k):
         return pl.ds(pl.multiple_of(chunk * k, chunk), chunk)
 
-    back, back_mate = [], []
+    back_mate = []
+    back = {
+        (a, g, offset): []
+        for a in (1, 0, 2)
+        for g in range(own_blocks)
+        for offset in (2, 1, 3, 0)
+        if a != 1 or offset
+    }
     for g in range(own_blocks):
         stacked = stack(solve(g))
-        these = slice(g * BLK, (g + 1) * BLK)
-        for b in range(3):
+        these = pl.ds(g * BLK, BLK)
+        for b in (1, 0, 2):
             total = None
             for a in (0, 1, 2):
                 if abs(a - b) > 1:
@@ -494,32 +517,32 @@
                 )
                 total = term if total is None else total + term
             rows_v[b, these] = mask_b[these, b * slab : (b + 1) * slab] * total
-        these = pl.ds(g * BLK, BLK)
-        for offset in (2, 1, 3, 0):
-            target = lax.rem(col + offset, cols)
-            origin = lax.rem(col + cols - offset, cols)
-            for a, span, device in ((0, (1, 2), above), (2, (0, 2), below)):
-                copy = send(
-                    rows_v.at[pl.ds(*span), these, lanes_of(target)],
-                    back_v.at[a, pl.ds(*spans[a]), col, space, these],
-                    {"rows": device, "cols": target},
-                )
-                back.append((a, g, origin, copy))
-        for offset in (2, 1, 3):
-            target = lax.rem(col + offset, cols)
-            origin = lax.rem(col + cols - offset, cols)
-            copy = send(
-                rows_v.at[:, these, lanes_of(target)],
-                back_v.at[1, :, col, space, these],
-                {"cols": target},
-            )
-            back.append((1, g, origin, copy))
+            for offset in (2, 1, 3, 0):
+                target = lax.rem(col + offset, cols)
+                source = rows_v.at[b, these, lanes_of(target)]
+                if b > 0:
+                    target_ref = back_v.at[0, b - 1, col, space, these]
+                    device = {"rows": above, "cols": target}
+                    back[0, g, offset].append(send(source, target_ref, device))
+                if b < 2:
+                    target_ref = back_v.at[2, b + 1, col, space, these]
+                    device = {"rows": below, "cols": target}
+                    back[2, g, offset].append(send(source, target_ref, device))
+            for offset in (2, 1, 3):
+                target = lax.rem(col + offset, cols)
+                source = rows_v.at[b, these, lanes_of(target)]
+                target_ref = back_v.at[1, b, col, space, these]
+                back[1, g, offset].append(send(source, target_ref, {"cols": target}))
         back_mate.append(
             send(rows_v.at[:, these, lanes], back_v.at[1, :, col, space, these], mate)
         )
     back_v[1, :, col, space] = rows_v[:, :, lanes]
-    for a, g, origin, copy in sorted(back, key=lambda item: (item[0] != 1, item[1])):
-        copy.wait_recv()
+    for (a, g, offset), copies in sorted(
+        back.items(), key=lambda item: (item[0][0] != 1, item[0][1])
+    ):
+        for copy in copies:
+            copy.wait_recv()
+        origin = lax.rem(col + cols - offset, cols)
         piece = back_v.at[a, pl.ds(*spans[a]), origin, space, pl.ds(g * BLK, BLK)]
         back_mate.append(send(piece, piece, mate))
         if len(back_mate) == own_blocks * cols:
@@ -589,12 +612,9 @@
             jax.ShapeDtypeStruct((own,), F32),
         ],
         in_specs=[
-            pl.BlockSpec(memory_space=pltpu.SMEM),
-            pl.BlockSpec(memory_space=pltpu.SMEM),
             pl.BlockSpec(memory_space=pltpu.HBM),
-            pl.BlockSpec(memory_space=pltpu.HBM),
-            pl.BlockSpec(memory_space=pltpu.VMEM),
-        ],
+        ]
+        * 5,
         out_specs=[pl.BlockSpec(memory_space=pltpu.VMEM)] * 2,
         scratch_shapes=[
             vmem((slab, window), F32),
@@ -616,9 +636,13 @@
             vmem((3, own, slab), F32),
             vmem((cols, 3, own, chunk), F32),
             vmem((cols, 3, own, chunk), F32),
-            pltpu.SemaphoreType.DMA((2,)),
-            pltpu.SemaphoreType.DMA((200,)),
-            pltpu.SemaphoreType.DMA((200,)),
+            pltpu.VMEM(pattern.T.shape, jnp.int32),
+            pltpu.SMEM(sub_blocks.shape, jnp.int32),
+            pltpu.SMEM(sub_count.shape, jnp.int32),
+            pltpu.SMEM((5, own_blocks, maxb), jnp.int32),
+            pltpu.SemaphoreType.DMA((5,)),
+            pltpu.SemaphoreType.DMA((240,)),
+            pltpu.SemaphoreType.DMA((240,)),
         ],
         compiler_params=pltpu.CompilerParams(
             collective_id=1, has_side_effects=True, vmem_limit_bytes=62 * 2**20

time: 108 us -> 104 us (0.963)
  Pallas kernels: 107 us -> 103 us
    pallas_call x1, Pallas kernels: 105 us -> 102 us  [shards(): pl.pallas_call(kernel, out_shape=[jax.ShapeDtypeStruct((own, window), F32...]
where the time goes in v3:
time: 104 us
  Pallas kernels  103 us (99%)
    pallas_call x1, Pallas kernels, shards(): pl.pallas_call(kernel, out_shape=[jax.ShapeDtypeStruct((own, window), F32...  102 us

profile of v3, /device:TPU:0, one launch (start us, length us, event | category | flops | bytes accessed | tf_op | source)
XLA Modules:
  0.0 104.2 jit_solution(13174208936333787557)
XLA Ops:
  0.6 101.6 %shard_map.68 = (f32[64,1536]{1,0:T(8,128)}, f32[64]{0:T(128)}) custom-call(s32[2,16]{1,0:T(2,128)} %pos_in.1, s32[2]{0:T(128)} %count_in.1, f32[64,1536]{1,0:T(8,128)} %ham_ref.1, f32[512,1536]{1,0:T(8,128)} %root_ref.1, s32[48,64]{1,0:T(8,128)} %bitcast.1), custom_call_target="tpu_custom_call" | custom-call | tf_op jit(solution)/shard_map/pallas_call | solution.py:608
  102.2 1.8 %shard_map.69 = (f32[64,1536]{1,0:T(8,128)}, f32[64]{0:T(128)}) custom-call(f32[64,1536]{1,0:T(8,128)} %get-tuple-element.4.density_ref, f32[64]{0:T(128)} %get-tuple-element.5.charges_ref), custom_call_target="tpu_custom_call" | custom-call | tf_op jit(solution)/shard_map/pallas_call | solution.py:651

commit v4 on v3

--- a/solution.py
+++ b/solution.py
@@ -351,25 +351,30 @@
 
     spans = {0: (0, 2), 1: (0, 3), 2: (1, 2)}
 
-    def region(a, k, part=None, span=None):
+    def region(a, k, b, part=None):
         size = half // BLK if part is None else half // BLK // 2
         start = 0 if part is None else part * size
-        return ortho_v.at[a, pl.ds(*(span or spans[a])), space, pl.ds(start, size), k]
-
-    def pass_on(a, k, part, device):
-        return send(region(a, k, part), region(a, k, part), device)
-
-    def to_rows(k, part):
-        return (
-            send(region(1, k, part, (1, 2)), region(0, k, part), up),
-            send(region(1, k, part, (0, 2)), region(2, k, part), down),
-        )
-
+        return ortho_v.at[a, b, space, pl.ds(start, size), k]
+
+    def pass_on(a, k, b, part, device):
+        return send(region(a, k, b, part), region(a, k, b, part), device)
+
+    def to_rows(k, b, part):
+        copies = []
+        if b > 0:
+            copies.append((0, b - 1, send(region(1, k, b, part), region(0, k, b - 1, part), up)))
+        if b < 2:
+            copies.append((2, b + 1, send(region(1, k, b, part), region(2, k, b + 1, part), down)))
+        return copies
+
+    panels = (1, 0, 2)
     pending = []
-    own_rows_out = to_rows(col, None)
-    own_first = pass_on(1, col, None, side)
-    own_second = pass_on(1, col, None, cross)
-    pending.append(pass_on(1, col, None, mate))
+    own_rows_out, own_first, own_second = {}, {}, {}
+    for b in panels:
+        own_rows_out[b] = to_rows(col, b, None)
+        own_first[b] = pass_on(1, col, b, None, side)
+        own_second[b] = pass_on(1, col, b, None, cross)
+        pending.append(pass_on(1, col, b, None, mate))
     for copy in relays:
         copy.wait_recv()
     for piece in order_of_pieces:
@@ -381,34 +386,36 @@
         b = (0, 1, 2, 1)[piece]
         wide_hi[a, b], wide_lo[a, b] = split(land_v[piece // 2, piece % 2])
 
-    own_first.wait_recv()
-    diagonal_a = pass_on(1, first, 1, cross)
-    first_rows = to_rows(first, 0)
-    pending.append(pass_on(1, first, None, mate))
-    own_second.wait_recv()
-    diagonal_b = pass_on(1, second, 0, side)
-    second_rows = to_rows(second, 1)
-    pending.append(pass_on(1, second, None, mate))
-    hops = []
-    for a, copy in ((0, own_rows_out[0]), (2, own_rows_out[1])):
+    hops, diagonals, first_rows, second_rows = [], {}, {}, {}
+    for b in panels:
+        own_first[b].wait_recv()
+        first_rows[b] = to_rows(first, b, 0)
+        diagonal_a = pass_on(1, first, b, 1, cross)
+        pending.append(pass_on(1, first, b, None, mate))
+        own_second[b].wait_recv()
+        second_rows[b] = to_rows(second, b, 1)
+        diagonals[b] = (diagonal_a, pass_on(1, second, b, 0, side))
+        pending.append(pass_on(1, second, b, None, mate))
+        for a, place, copy in own_rows_out[b]:
+            copy.wait_recv()
+            hops.append((a, first, place, 1, pass_on(a, col, place, 1, side)))
+            hops.append((a, second, place, 0, pass_on(a, col, place, 0, cross)))
+            pending.append(pass_on(a, col, place, None, mate))
+    for b in panels:
+        for copy in diagonals[b]:
+            copy.wait_recv()
+        pending.append(pass_on(1, third, b, None, mate))
+        for a, place, copy in first_rows[b]:
+            copy.wait_recv()
+            hops.append((a, third, place, 0, pass_on(a, first, place, 0, cross)))
+            pending.append(pass_on(a, first, place, 0, mate))
+        for a, place, copy in second_rows[b]:
+            copy.wait_recv()
+            hops.append((a, third, place, 1, pass_on(a, second, place, 1, side)))
+            pending.append(pass_on(a, second, place, 1, mate))
+    for a, k, place, part, copy in hops:
         copy.wait_recv()
-        hops.append((a, first, 1, pass_on(a, col, 1, side)))
-        hops.append((a, second, 0, pass_on(a, col, 0, cross)))
-        pending.append(pass_on(a, col, None, mate))
-    diagonal_a.wait_recv()
-    diagonal_b.wait_recv()
-    pending.append(pass_on(1, third, None, mate))
-    for a, copy in ((0, first_rows[0]), (2, first_rows[1])):
-        copy.wait_recv()
-        hops.append((a, third, 0, pass_on(a, first, 0, cross)))
-        pending.append(pass_on(a, first, 0, mate))
-    for a, copy in ((0, second_rows[0]), (2, second_rows[1])):
-        copy.wait_recv()
-        hops.append((a, third, 1, pass_on(a, second, 1, side)))
-        pending.append(pass_on(a, second, 1, mate))
-    for a, k, part, copy in hops:
-        copy.wait_recv()
-        pending.append(pass_on(a, k, part, mate))
+        pending.append(pass_on(a, k, place, part, mate))
     for copy in pending:
         copy.wait_recv()
 
@@ -641,8 +648,8 @@
             pltpu.SMEM(sub_count.shape, jnp.int32),
             pltpu.SMEM((5, own_blocks, maxb), jnp.int32),
             pltpu.SemaphoreType.DMA((5,)),
-            pltpu.SemaphoreType.DMA((240,)),
-            pltpu.SemaphoreType.DMA((240,)),
+            pltpu.SemaphoreType.DMA((320,)),
+            pltpu.SemaphoreType.DMA((320,)),
         ],
         compiler_params=pltpu.CompilerParams(
             collective_id=1, has_side_effects=True, vmem_limit_bytes=62 * 2**20

time: 104 us -> 103 us (level)
    pallas_call x1, Pallas kernels: 102 us -> 100 us  [shards(): pl.pallas_call(kernel, out_shape=[jax.ShapeDtypeStruct((own, window), F32...]
where the time goes in v4:
time: 103 us
  Pallas kernels  102 us (99%)
    pallas_call x1, Pallas kernels, shards(): pl.pallas_call(kernel, out_shape=[jax.ShapeDtypeStruct((own, window), F32...  100 us

profile of v4, /device:TPU:0, one launch (start us, length us, event | category | flops | bytes accessed | tf_op | source)
XLA Modules:
  0.0 102.8 jit_solution(15657856085029233065)
XLA Ops:
  0.6 100.3 %shard_map.68 = (f32[64,1536]{1,0:T(8,128)}, f32[64]{0:T(128)}) custom-call(s32[2,16]{1,0:T(2,128)} %pos_in.1, s32[2]{0:T(128)} %count_in.1, f32[64,1536]{1,0:T(8,128)} %ham_ref.1, f32[512,1536]{1,0:T(8,128)} %root_ref.1, s32[48,64]{1,0:T(8,128)} %bitcast.1), custom_call_target="tpu_custom_call" | custom-call | tf_op jit(solution)/shard_map/pallas_call | solution.py:615
  100.9 1.8 %shard_map.69 = (f32[64,1536]{1,0:T(8,128)}, f32[64]{0:T(128)}) custom-call(f32[64,1536]{1,0:T(8,128)} %get-tuple-element.4.density_ref, f32[64]{0:T(128)} %get-tuple-element.5.charges_ref), custom_call_target="tpu_custom_call" | custom-call | tf_op jit(solution)/shard_map/pallas_call | solution.py:658

commit v5 on v4

--- a/solution.py
+++ b/solution.py
@@ -24,6 +24,8 @@
 def product(stacked, right):
     high, low = right
     half = stacked.shape[0] // 2
+    if half >= 256:
+        return dot(stacked[:half], high) + dot(stacked[half:], high) + dot(stacked[:half], low)
     both = dot(stacked, high)
     return both[:half] + both[half:] + dot(stacked[:half], low)
 
@@ -558,20 +560,20 @@
             acc_v[...] = product(left_block(1), window_block(back_v, 1))
     for other in back_mate[own_blocks * cols :]:
         other.wait_recv()
-    done = combine(
-        product(left_block(0), window_block(back_v, 0)),
-        acc_v[...],
-        product(left_block(2), window_block(back_v, 2)),
-        chunk,
-    )
-    for b in range(3):
-        masked = mask_a[:, :, b * chunk : (b + 1) * chunk].reshape(half, chunk)
-        piece = masked * done[:, b * chunk : (b + 1) * chunk]
-        strip_v[:, b] = piece.reshape(cols, own, chunk)
+    outer = [window_block(back_v, a) for a in (0, 2)]
     outs = []
-    for offset in (2, 1, 3):
+    for offset in (2, 1, 3, 0):
         target = lax.rem(col + offset, cols)
-        outs.append(send(strip_v.at[target], final_v.at[col], {"cols": target}))
+        rows = pl.ds(pl.multiple_of(target * own, own), own)
+        terms = [
+            product(left_s[:, rows, a * slab : (a + 1) * slab].reshape(2 * own, slab), right)
+            for a, right in zip((0, 2), outer)
+        ]
+        done = mask_a[target] * combine(terms[0], acc_v[rows, :], terms[1], chunk)
+        for b in range(3):
+            strip_v[target, b] = done[:, b * chunk : (b + 1) * chunk]
+        if offset:
+            outs.append(send(strip_v.at[target], final_v.at[col], {"cols": target}))
     final_v[col] = strip_v[col]
     for copy in outs:
         copy.wait_recv()

time: 103 us -> 103 us (level)
  no operation moved by 1% of the time
where the time goes in v5:
time: 103 us
  Pallas kernels  102 us (99%)
    pallas_call x1, Pallas kernels, shards(): pl.pallas_call(kernel, out_shape=[jax.ShapeDtypeStruct((own, window), F32...  100 us

profile of v5, /device:TPU:0, one launch (start us, length us, event | category | flops | bytes accessed | tf_op | source)
XLA Modules:
  0.0 102.7 jit_solution(6824554316069007888)
XLA Ops:
  0.6 100.1 %shard_map.68 = (f32[64,1536]{1,0:T(8,128)}, f32[64]{0:T(128)}) custom-call(s32[2,16]{1,0:T(2,128)} %pos_in.1, s32[2]{0:T(128)} %count_in.1, f32[64,1536]{1,0:T(8,128)} %ham_ref.1, f32[512,1536]{1,0:T(8,128)} %root_ref.1, s32[48,64]{1,0:T(8,128)} %bitcast.1), custom_call_target="tpu_custom_call" | custom-call | tf_op jit(solution)/shard_map/pallas_call | solution.py:617
  100.7 1.8 %shard_map.69 = (f32[64,1536]{1,0:T(8,128)}, f32[64]{0:T(128)}) custom-call(f32[64,1536]{1,0:T(8,128)} %get-tuple-element.4.density_ref, f32[64]{0:T(128)} %get-tuple-element.5.charges_ref), custom_call_target="tpu_custom_call" | custom-call | tf_op jit(solution)/shard_map/pallas_call | solution.py:660
